TPU v7x, 32 devices: a whole 2x2x4 slice. The times are simulated.
32 devices in a mesh: dp: 16 (over z, y, core), mp: 2 (over x).
Axes of the slice: x: 2, y: 2, z: 4, core: 2. Of those that a mesh axis runs over, the one named last changes fastest.
Arguments:
- bag_lengths: int32 [16, 2048], P('mp', 'dp'), may hold values from 1 to 8
- owners: int32 [16, 2048, 8, 1], P('mp', 'dp'), may hold values from 0 to 15; in each aligned block of 1024 rows (0 to 1023, 1024 to 2047, ..., all dimensions but the last counted through in order) at most 128 rows name the same one
- row_slots: int32 [16, 2048, 8], P('mp', 'dp'), may hold values from 0 to 511
- admit_mask: int32 [16, 2048, 8], P('mp', 'dp'), may hold values 0 or 1
- expired: int32 [16, 8192], P('mp', 'dp'), may hold values 0 or 1
- embeddings: float32 [16, 8192, 128], P('mp', 'dp'), may hold values from -3 to 3
- accumulator: float32 [16, 8192], P('mp', 'dp'), may hold values from 0.001 to 0.01
- hidden_weight: bfloat16 [2048, 1024], P(None, 'mp'), may hold values from -0.125 to 0.125
- output_weight: float32 [1024], P('mp'), may hold values from -0.9 to 0.9
- labels: int32 [2048], P('dp'), may hold values 0 or 1
Outputs:
- new_table: float32 [16, 8192, 128], P('mp', 'dp')
- new_accum: float32 [16, 8192], P('mp', 'dp')
- weight_grad: bfloat16 [2048, 1024], P(None, 'mp')
- logits: float32 [2048], P('dp')
Inputs may be any that keep to these rules, and one draw needn't show every extreme that they name: Among the 128 x 8 lookups of one index of dp into one table (aligned blocks of owners' rows), at most 128 name the same owner; in some blocks one owner is named exactly 128 times.
All inputs are finite; a program needn't handle non-finite values. No bound on the sum of `admit_mask` or of `expired` or of `labels` on one device may be relied on, other than what follows from the above.
Results may differ from a plain program's by a relative error of at most 0.0085.
Values may be sent and summed in bfloat16 or wider, within the bound.
A program may use at most 64 MiB of HBM per device.

v0:
```python
import jax
import jax.numpy as jnp
from jax import lax
from jax.sharding import PartitionSpec as P

LEARN_RATE = 0.05
ACC_RESET = 0.001


def silu_slope(preact):
    sig = jax.nn.sigmoid(preact)
    return sig * (1.0 + preact * (1.0 - sig))


def shards(
    bag_lengths,
    owners,
    row_slots,
    admit_mask,
    expired,
    embeddings,
    accumulator,
    hidden_weight,
    output_weight,
    labels,
):
    groups = lax.axis_size("dp")
    tab_dev, tok_dev, bag_size = row_slots.shape
    rows_dev = embeddings.shape[1]
    row_width = embeddings.shape[2]
    lookups = tok_dev * bag_size
    capacity = 2 * lookups // groups
    buffer_len = groups * capacity
    places = jnp.arange(bag_size, dtype=jnp.int32)
    live_mask = ((places[None, None, :] < bag_lengths[:, :, None]) & (admit_mask == 1)).astype(
        jnp.float32
    )
    counted = jnp.sum(live_mask, axis=2)
    bag_weight = live_mask / jnp.maximum(counted, 1.0)[:, :, None]
    target = owners[..., 0].reshape(tab_dev, lookups)
    lookup_ids = jnp.arange(lookups, dtype=jnp.int32)
    earlier = lookup_ids[None, :] < lookup_ids[:, None]
    same_owner = target[:, :, None] == target[:, None, :]
    ranked = jnp.sum((same_owner & earlier[None, :, :]).astype(jnp.int32), axis=2)
    placed = target * capacity + ranked
    slot_ids = jnp.arange(buffer_len, dtype=jnp.int32)
    hits = placed[:, :, None] == slot_ids[None, None, :]
    flat_slots = row_slots.reshape(tab_dev, lookups)
    request = jnp.sum(jnp.where(hits, flat_slots[:, :, None], 0), axis=1)
    sample_of = lookup_ids // bag_size
    slot_sample = jnp.sum(jnp.where(hits, sample_of[None, :, None], 0), axis=1)
    flat_weight = bag_weight.reshape(tab_dev, lookups)
    slot_weight = jnp.sum(jnp.where(hits, flat_weight[:, :, None], jnp.float32(0.0)), axis=1)
    pool_matrix = jnp.sum(
        jnp.where(
            hits.reshape(tab_dev, tok_dev, bag_size, buffer_len),
            bag_weight[:, :, :, None],
            jnp.float32(0.0),
        ),
        axis=2,
    )
    request = request.reshape(tab_dev, groups, capacity)
    arrived = lax.all_to_all(request, "dp", split_axis=1, concat_axis=1, tiled=True)
    fresh_rows = jnp.where(expired[:, :, None] == 1, jnp.float32(0.0), embeddings)
    fresh_acc = jnp.where(expired == 1, jnp.float32(ACC_RESET), accumulator)
    row_pick = (
        arrived.reshape(tab_dev, buffer_len)[:, :, None]
        == jnp.arange(rows_dev, dtype=jnp.int32)[None, None, :]
    ).astype(jnp.bfloat16)
    fetched = jnp.einsum(
        "tbr,tre->tbe",
        row_pick,
        fresh_rows.astype(jnp.bfloat16),
        preferred_element_type=jnp.float32,
    ).astype(jnp.bfloat16)
    fetched = fetched.reshape(tab_dev, groups, capacity, row_width)
    returned = lax.all_to_all(fetched, "dp", split_axis=1, concat_axis=1, tiled=True)
    returned_rows = returned.reshape(tab_dev, buffer_len, row_width).astype(jnp.float32)
    pooled = jnp.einsum("tnb,tbe->tne", pool_matrix, returned_rows, precision=lax.Precision.HIGHEST)
    features = pooled.transpose(1, 0, 2).reshape(tok_dev, tab_dev * row_width).astype(jnp.bfloat16)
    portion = lax.all_gather(features, "mp", axis=1, tiled=True)
    summed_pre = jnp.dot(portion, hidden_weight, preferred_element_type=jnp.float32)
    hidden = jax.nn.silu(summed_pre).astype(jnp.bfloat16)
    logits = lax.psum(jnp.sum(hidden.astype(jnp.float32) * output_weight, axis=1), "mp")
    dlogit = jax.nn.sigmoid(logits) - labels.astype(jnp.float32)
    dhidden = (dlogit[:, None] * output_weight * silu_slope(summed_pre)).astype(jnp.bfloat16)
    feature_grad = lax.psum_scatter(
        lax.dot_general(
            hidden_weight, dhidden, (((1,), (1,)), ((), ())), preferred_element_type=jnp.float32
        ).astype(jnp.bfloat16),
        "mp",
        scatter_dimension=0,
        tiled=True,
    ).astype(jnp.float32)
    per_table = feature_grad.reshape(tab_dev, row_width, tok_dev).transpose(0, 2, 1)
    sample_pick = (
        slot_sample[:, :, None] == jnp.arange(tok_dev, dtype=jnp.int32)[None, None, :]
    ).astype(jnp.float32)
    slot_grad = jnp.einsum("tbn,tne->tbe", sample_pick, per_table, precision=lax.Precision.HIGHEST)
    outgoing = (slot_weight[:, :, None] * slot_grad).astype(jnp.bfloat16)
    outgoing = outgoing.reshape(tab_dev, groups, capacity, row_width)
    grad_part = lax.all_to_all(outgoing, "dp", split_axis=1, concat_axis=1, tiled=True)
    slot_part = lax.all_to_all(request, "dp", split_axis=1, concat_axis=1, tiled=True)
    items = grad_part.shape[0]
    selector = (
        slot_part.reshape(items, -1)[:, :, None] == jnp.arange(rows_dev, dtype=jnp.int32)
    ).astype(jnp.bfloat16)
    summed = jnp.einsum(
        "ksr,kse->kre",
        selector,
        grad_part.reshape(items, -1, row_width),
        preferred_element_type=jnp.float32,
    )
    new_acc = fresh_acc + jnp.mean(summed * summed, axis=2)
    new_rows = fresh_rows - LEARN_RATE * summed / jnp.sqrt(new_acc)[:, :, None]
    local_grad = lax.dot_general(
        portion, dhidden, (((0,), (0,)), ((), ())), preferred_element_type=jnp.float32
    )
    shared = lax.psum_scatter(local_grad, "dp", scatter_dimension=0, tiled=True).astype(
        jnp.bfloat16
    )
    weight_grad = lax.all_gather(shared, "dp", axis=0, tiled=True)
    return (new_rows, new_acc, weight_grad, logits)


def solution(mesh):
    in_specs = (
        P("mp", "dp"),
        P("mp", "dp", None, None),
        P("mp", "dp", None),
        P("mp", "dp", None),
        P("mp", "dp"),
        P("mp", "dp", None),
        P("mp", "dp"),
        P(None, "mp"),
        P("mp"),
        P("dp"),
    )
    out_specs = (P("mp", "dp", None), P("mp", "dp"), P(None, "mp"), P("dp"))
    return jax.shard_map(shards, mesh=mesh, in_specs=in_specs, out_specs=out_specs, check_vma=False)
```

profile of v0, /device:TPU:15, one launch (start us, length us, event | category | flops | bytes accessed | tf_op | source)
XLA Modules:
  0.0 399.5 jit_solution(10938816243787522423)
XLA Ops:
  7.2 0.0 copy-start
  7.2 1.3 iota_compare_fusion.7
  8.5 0.0 copy-start.3
  8.5 1.0 copy.47
  9.4 0.3 reshape_squeeze.3
  9.7 7.8 %convert_reduce_fusion = s32[8,1024]{1,0:T(8,128)S(1)} fusion(s32[8,1024]{1,0:T(8,128)S(1)} %reshape_squeeze.3, pred[1024,1024]{1,0:T(8,128)(4,1)} %iota_compare_fusion.7), kind=kLoop, calls=%fused_computation.9 | loop fusion | flops 33546240 | bytes 1114112 | tf_op jit(solution)/shard_map/reduce_sum | solution.py:44
  17.6 1.0 copy.48
  18.5 0.3 broadcast_in_dim.88
  18.8 33.8 %select_reduce_fusion.1 = (s32[8,2048]{1,0:T(8,128)}, s32[8,2048]{1,0:T(8,128)}) fusion(s32[1024]{0:T(1024)S(1)} %add_select_fusion, s32[8,1024]{1,0:T(8,128)S(1)} %multiply_add_fusion, s32[8,1024]{1,0:T(8,128)S(1)} %broadcast_in_dim.88), kind=kLoop, calls=%fused_computation.2 | loop fusion | flops 83853312 | bytes 200704 | tf_op jit(solution)/shard_map/reduce_sum | solution.py:51
  52.6 6.5 %all-to-all-start = ((s32[8,16,128]{2,0,1:T(8,128)}), s32[8,16,128]{2,0,1:T(8,128)S(1)}, u32[]{:S(2)}, u32[]{:S(2)}) async-start(s32[8,16,128]{2,0,1:T(8,128)} %bitcast), calls=%async_computation | async-start | bytes 131072 | tf_op jit(solution)/shard_map/all_to_all | solution.py:103
  59.1 2.9 copy.46
  62.0 0.0 copy-done.3
  62.0 1.4 all-to-all-done
  63.4 7.7 %fusion.6 = bf16[8,2048,128]{2,1,0:T(8,128)(2,1)S(1)} fusion(s32[8,2048]{1,0:T(8,128)S(1)} %bitcast.36, f32[8,512,128]{1,2,0:T(8,128)} %copy.46, pred[8,512]{1,0:T(8,128)(4,1)S(1)} %broadcast_compare_fusion), kind=kOutput, calls=%fused_computation.17 | convolution fusion | flops 2158493696 | bytes 6361088 | tf_op jit(solution)/shard_map/tbr,tre->tbe/dot_general | solution.py:70
  71.2 2.3 copy.53
  73.4 0.0 copy-start.4
  73.4 7.2 %all-to-all-start.1 = ((bf16[8,16,128,128]{3,2,0,1:T(8,128)(2,1)}), bf16[8,16,128,128]{3,2,0,1:T(8,128)(2,1)}, u32[]{:S(2)}, u32[]{:S(2)}) async-start(bf16[8,16,128,128]{3,2,0,1:T(8,128)(2,1)} %copy.53), calls=%async_computation.1 | async-start | bytes 8388608 | tf_op jit(solution)/shard_map/all_to_all | solution.py:77
  80.6 0.2 reduce-scatter.3.cloned.1.call-start
  80.8 1.1 reduce_sum.79
  81.9 0.0 copy-done.4
  81.9 0.0 copy-done.6
  82.0 0.2 copy.49
  82.2 1.9 bitcast_add_fusion
  84.1 27.1 %select_reduce_fusion = f32[8,128,2048]{2,1,0:T(8,128)} fusion(f32[8,128,8]{2,1,0:T(8,128)S(1)} %copy.49, s32[8,128,8]{2,1,0:T(8,128)} %bitcast_add_fusion), kind=kLoop, calls=%fused_computation | loop fusion | flops 48234496 | bytes 8454144 | tf_op jit(solution)/shard_map/reduce_sum | solution.py:54
  111.2 61.9 %all-to-all-done.1 = bf16[8,16,128,128]{3,2,0,1:T(8,128)(2,1)} async-done(((bf16[8,16,128,128]{3,2,0,1:T(8,128)(2,1)}), bf16[8,16,128,128]{3,2,0,1:T(8,128)(2,1)}, u32[]{:S(2)}, u32[]{:S(2)}) %all-to-all-start.1) | async-done | bytes 4194336 | tf_op jit(solution)/shard_map/all_to_all | solution.py:77
  173.1 6.8 %copy.54 = bf16[8,16,128,128]{2,1,3,0:T(8,128)(2,1)} copy(bf16[8,16,128,128]{3,2,0,1:T(8,128)(2,1)} %all-to-all-done.1) | data formatting | bytes 8388608 | tf_op jit(solution)/shard_map/all_to_all | solution.py:77
  179.9 7.3 %reshape.87 = bf16[8,2048,128]{1,2,0:T(8,128)(2,1)} reshape(bf16[8,16,128,128]{2,1,3,0:T(8,128)(2,1)} %copy.54) | data formatting | bytes 8388608 | tf_op jit(solution)/shard_map/reshape | solution.py:78
  187.2 8.8 %convolution_convert_fusion.1 = bf16[8,128,128]{1,2,0:T(8,128)(2,1)S(1)} fusion(f32[8,128,2048]{2,1,0:T(8,128)} %select_reduce_fusion, bf16[8,2048,128]{1,2,0:T(8,128)(2,1)} %reshape.87), kind=kOutput, calls=%fused_computation.23 | convolution fusion | flops 3221356544 | bytes 12845056 | tf_op jit(solution)/shard_map/tnb,tbe->tne/dot_general | solution.py:79
  196.0 8.4 %all_gather.6 = bf16[128,2048]{0,1:T(8,128)(2,1)S(1)} all-gather(bf16[128,1024]{0,1:T(8,128)(2,1)S(1)} %bitcast.34), channel_id=1, replica_groups=mesh['dp'=16,'mp'=2] {'mp'}, dimensions={1}, use_global_device_ids=true | all-gather | bytes 786432 | tf_op jit(solution)/shard_map/all_gather | solution.py:81
  204.4 0.0 copy-done
  204.4 0.0 copy-done.7
  204.4 0.6 multiply_reduce_fusion.1
  205.0 3.8 psum.7
  208.8 0.0 copy-done.8
  208.8 1.6 fusion.7
  210.4 0.0 reduce-scatter.3.cloned.1.call-update
  210.4 0.0 reduce-scatter.5.cloned.1.call-start
  210.5 0.3 broadcast_in_dim.91
  210.8 2.8 fusion.15
  213.5 0.0 copy-done.9
  213.5 0.0 reduce-scatter.5.cloned.1.call-update
  213.6 9.9 %select_reduce_fusion.2 = f32[8,2048]{1,0:T(8,128)S(1)} fusion(f32[8,1024]{1,0:T(8,128)S(1)} %broadcast_in_dim.91, s32[8,1024]{1,0:T(8,128)S(1)} %multiply_add_fusion), kind=kLoop, calls=%fused_computation.3 | loop fusion | flops 50315264 | bytes 131072 | tf_op jit(solution)/shard_map/reduce_sum | solution.py:53
  223.5 2.0 reduce-scatter.3.cloned.1.call-done
  225.5 1.1 copy.60
  226.6 0.0 copy-done.10
  226.6 5.8 %multiply_convert_fusion = bf16[8,2048,128]{2,1,0:T(8,128)(2,1)S(1)} fusion(f32[8,2048]{1,0:T(8,128)S(1)} %select_reduce_fusion.2, bf16[8,128,128]{2,1,0:T(8,128)(2,1)S(1)} %bitcast.35, s32[8,2048]{1,0:T(8,128)S(1)} %copy-done.10), kind=kOutput, calls=%fused_computation.12 | convolution fusion | flops 543162368 | bytes 4587520 | tf_op jit(solution)/shard_map/tbn,tne->tbe/dot_general | solution.py:99
  232.4 2.3 copy.56
  234.7 6.5 %all-to-all-start.2 = ((bf16[8,16,128,128]{3,2,0,1:T(8,128)(2,1)}), bf16[8,16,128,128]{3,2,0,1:T(8,128)(2,1)}, u32[]{:S(2)}, u32[]{:S(2)}) async-start(bf16[8,16,128,128]{3,2,0,1:T(8,128)(2,1)} %copy.56), calls=%async_computation.3 | async-start | bytes 8388608 | tf_op jit(solution)/shard_map/all_to_all | solution.py:102
  241.2 0.3 all-gather.2.cloned.1.call-start
  241.5 105.5 %reduce-scatter.5.cloned.1.call-done = f32[128,512]{1,0:T(8,128)} async-done(((f32[2048,512]{1,0:T(8,128)}), f32[128,512]{1,0:T(8,128)}) %reduce-scatter.5.cloned.1.call-update) | async-done | bytes 262160 | tf_op jit(solution)/shard_map/reduce_scatter | solution.py:119
  347.0 1.6 convert_element_type.64
  348.6 0.0 all-gather.2.cloned.1.call-update
  348.6 10.3 %all-to-all-done.2 = bf16[8,16,128,128]{3,2,0,1:T(8,128)(2,1)} async-done(((bf16[8,16,128,128]{3,2,0,1:T(8,128)(2,1)}), bf16[8,16,128,128]{3,2,0,1:T(8,128)(2,1)}, u32[]{:S(2)}, u32[]{:S(2)}) %all-to-all-start.2) | async-done | bytes 4194336 | tf_op jit(solution)/shard_map/all_to_all | solution.py:102
  358.9 6.8 %copy.57 = bf16[8,16,128,128]{2,1,3,0:T(8,128)(2,1)} copy(bf16[8,16,128,128]{3,2,0,1:T(8,128)(2,1)} %all-to-all-done.2) | data formatting | bytes 8388608 | tf_op jit(solution)/shard_map/all_to_all | solution.py:102
  365.7 7.3 %reshape.90 = bf16[8,2048,128]{1,2,0:T(8,128)(2,1)} reshape(bf16[8,16,128,128]{2,1,3,0:T(8,128)(2,1)} %copy.57) | data formatting | bytes 8388608 | tf_op jit(solution)/shard_map/reshape | solution.py:111
  373.1 8.8 %multiply_reduce_fusion = (f32[8,512]{1,0:T(8,128)S(1)}, f32[8,512,128]{1,2,0:T(8,128)S(1)}) fusion(bf16[8,2048,128]{1,2,0:T(8,128)(2,1)} %reshape.90, s32[8,2048]{1,0:T(8,128)S(1)} %bitcast.37), kind=kOutput, calls=%fused_computation.21 | convolution fusion | flops 2156916736 | bytes 6373376 | tf_op jit(solution)/shard_map/ksr,kse->kre/dot_general | solution.py:108
  381.9 0.0 copy-done.5
  381.9 0.6 fusion.16
  382.5 0.0 copy-done.2
  382.5 1.9 divide_subtract_fusion
  384.5 2.9 copy.58
  387.4 2.5 all-gather.2.cloned.1.call-done
  389.9 3.0 copy.62
  392.9 0.0 copy-done.1
  (15 shorter events, 0.1 us)
Async XLA Ops:
  7.2 197.2 %copy-start = (bf16[2048,512]{1,0:T(8,128)(2,1)S(1)}, bf16[2048,512]{1,0:T(8,128)(2,1)}, u32[]{:S(2)}) copy-start(bf16[2048,512]{1,0:T(8,128)(2,1)} %param.17) | copy-start | bytes 6291460
  8.5 53.6 %copy-start.3 = (s32[8,512]{1,0:T(8,128)S(1)}, s32[8,512]{1,0:T(8,128)}, u32[]{:S(2)}) copy-start(s32[8,512]{1,0:T(8,128)} %param.14) | copy-start | bytes 49156
  52.6 10.8 %all-to-all-start = ((s32[8,16,128]{2,0,1:T(8,128)}), s32[8,16,128]{2,0,1:T(8,128)S(1)}, u32[]{:S(2)}, u32[]{:S(2)}) async-start(s32[8,16,128]{2,0,1:T(8,128)} %bitcast), calls=%async_computation | async-start | bytes 131072 | tf_op jit(solution)/shard_map/all_to_all | solution.py:103
  73.4 8.5 %copy-start.4 = (s32[8,128,8]{1,2,0:T(8,128)S(1)}, s32[8,128,8]{1,2,0:T(8,128)}, u32[]{:S(2)}) copy-start(s32[8,128,8]{1,2,0:T(8,128)} %param.13) | copy-start | bytes 98308
  73.4 8.5 %copy-start.6 = (s32[8,128]{1,0:T(8,128)S(1)}, s32[8,128]{1,0:T(8,128)}, u32[]{:S(2)}) copy-start(s32[8,128]{1,0:T(8,128)} %param.10) | copy-start | bytes 12292
  73.4 99.6 %all-to-all-start.1 = ((bf16[8,16,128,128]{3,2,0,1:T(8,128)(2,1)}), bf16[8,16,128,128]{3,2,0,1:T(8,128)(2,1)}, u32[]{:S(2)}, u32[]{:S(2)}) async-start(bf16[8,16,128,128]{3,2,0,1:T(8,128)(2,1)} %copy.53), calls=%async_computation.1 | async-start | bytes 8388608 | tf_op jit(solution)/shard_map/all_to_all | solution.py:77
  80.6 144.9 %reduce-scatter.3.cloned.1.call-start = ((), (), s32[]{:S(2)}) async-start(), calls=%async_computation.5 | async-start | bytes 786432 | tf_op jit(solution)/shard_map/reduce_scatter | solution.py:87
  187.2 17.2 %copy-start.7 = (f32[512]{0:T(512)S(1)}, f32[512]{0:T(512)}, u32[]{:S(2)}) copy-start(f32[512]{0:T(512)} %param.18) | copy-start | bytes 6148
  187.2 21.6 %copy-start.8 = (s32[128]{0:T(128)S(1)}, s32[128]{0:T(128)}, u32[]{:S(2)}) copy-start(s32[128]{0:T(128)} %param.19) | copy-start | bytes 1540
  208.8 4.8 %copy-start.9 = (f32[128]{0:T(128)}, f32[128]{0:T(128)S(1)}, u32[]{:S(2)}) copy-start(f32[128]{0:T(128)S(1)} %psum.7) | copy-start | bytes 1540
  210.4 136.6 %reduce-scatter.5.cloned.1.call-start = ((), (), s32[]{:S(2)}) async-start(), calls=%async_computation.6 | async-start | bytes 4456448 | tf_op jit(solution)/shard_map/reduce_scatter | solution.py:119
  210.8 15.9 %copy-start.10 = (s32[8,2048]{1,0:T(8,128)S(1)}, s32[8,2048]{1,0:T(8,128)}, u32[]{:S(2)}) copy-start(s32[8,2048]{1,0:T(8,128)} %get-tuple-element.20) | copy-start | bytes 196612
  234.7 124.2 %all-to-all-start.2 = ((bf16[8,16,128,128]{3,2,0,1:T(8,128)(2,1)}), bf16[8,16,128,128]{3,2,0,1:T(8,128)(2,1)}, u32[]{:S(2)}, u32[]{:S(2)}) async-start(bf16[8,16,128,128]{3,2,0,1:T(8,128)(2,1)} %copy.56), calls=%async_computation.3 | async-start | bytes 8388608 | tf_op jit(solution)/shard_map/all_to_all | solution.py:102
  241.2 148.7 %all-gather.2.cloned.1.call-start = ((), (), s32[]{:S(2)}) async-start(), calls=%async_computation.7 | async-start | bytes 2228224 | tf_op jit(solution)/shard_map/all_gather | solution.py:122
  373.1 8.8 %copy-start.5 = (f32[8,512]{1,0:T(8,128)S(1)}, f32[8,512]{1,0:T(8,128)}, u32[]{:S(2)}) copy-start(f32[8,512]{1,0:T(8,128)} %param.16) | copy-start | bytes 49156
  373.1 9.5 %copy-start.2 = (f32[8,512,128]{1,2,0:T(8,128)S(1)}, f32[8,512,128]{1,2,0:T(8,128)}, u32[]{:S(2)}) copy-start(f32[8,512,128]{1,2,0:T(8,128)} %copy.46) | copy-start | bytes 6291460
  382.5 10.4 %copy-start.1 = (bf16[2048,512]{1,0:T(8,128)(2,1)S(1)}, bf16[2048,512]{1,0:T(8,128)(2,1)}, u32[]{:S(2)}) copy-start(bf16[2048,512]{1,0:T(8,128)(2,1)} %param.17) | copy-start | bytes 6291460
Sparse Core Ops, SparseCore 0:
  210.6 14.8 reduce-scatter.2
  229.3 117.6 reduce-scatter.4
  349.2 40.6 all-gather.1
where the time goes:
time: 404 us; the launch traced here: 399 us
  waiting for transfers between devices  184 us (46%)
  other arithmetic  86.1 us (21%)
  local copies, waits for them, and re-layouts  46.8 us (12%)
  matrix products  36.1 us (9%)
  starting transfers between devices  20.7 us (5%)
  between operations  13.9 us (3%)
  blocking collectives  12.2 us (3%)
    reduce_scatter x1, waiting for transfers between devices, shards(): lax.psum_scatter(local_grad, 'dp', scatter_dimension=0, tiled=True)  106 us
    all_to_all x1, waiting for transfers between devices, shards(): lax.all_to_all(fetched, 'dp', split_axis=1, concat_axis=1, tiled=True)  61.9 us
    reduce_sum x1, other arithmetic, shards(): slot_sample = jnp.sum(jnp.where(hits, sample_of[None, :, None], 0), axis=1)  33.8 us
    reduce_sum x1, other arithmetic, shards(): jnp.sum(jnp.where(hits.reshape(tab_dev, tok_dev, bag_size, buffer_len), b...  27.1 us
    unnamed x27, local copies, waits for them, and re-layouts  10.8 us
    all_to_all x1, waiting for transfers between devices, shards(): lax.all_to_all(outgoing, 'dp', split_axis=1, concat_axis=1, tiled=True)  10.3 us
    reduce_sum x1, other arithmetic, shards(): jnp.sum(jnp.where(hits, flat_weight[:, :, None], jnp.float32(0.0)), axis=1)  9.93 us
    dot_general x1, matrix products, shards(): jnp.einsum('ksr,kse->kre', selector, grad_part.reshape(items, -1, row_wid...  8.84 us
  transfers between devices with their start and end apart: 6, of which 6 were waited for; matrix products, arithmetic and copies ran while one was open for 21% of the time, Pallas kernels for 0%

commit v1 on v0

v1 whole, which is shorter than its diff:
```python
import functools

import jax
import jax.numpy as jnp
from jax import lax
from jax.experimental import pallas as pl
from jax.experimental.pallas import tpu as pltpu
from jax.sharding import PartitionSpec as P

LEARN_RATE = 0.05
ACC_RESET = 0.001
MESH = pl.DeviceIdType.MESH
BASE = 256


def silu_slope(preact):
    sig = jax.nn.sigmoid(preact)
    return sig * (1.0 + preact * (1.0 - sig))


def push_kernel(axis, groups, dims, *refs):
    count = len(dims)
    ins, outs = refs[:count], refs[count : 2 * count]
    send_sem, recv_sem, local_sem = refs[2 * count :]
    me = lax.axis_index(axis)

    def block(ref, dim, index):
        return ref.at[index] if dim == 0 else ref.at[:, index]

    barrier = pltpu.get_barrier_semaphore()

    def greet(step, carry):
        peer = lax.rem(me + step, groups)
        pl.semaphore_signal(barrier, inc=1, device_id={axis: peer}, device_id_type=MESH)
        return carry

    lax.fori_loop(1, groups, greet, 0)
    pl.semaphore_wait(barrier, groups - 1)

    for item in range(count):
        dim = dims[item]

        def send(step, carry, item=item, dim=dim):
            peer = lax.rem(me + step, groups)
            source = ins[item] if dim is None else block(ins[item], dim, peer)
            pltpu.make_async_remote_copy(
                src_ref=source,
                dst_ref=block(outs[item], dim or 0, me),
                send_sem=send_sem.at[item],
                recv_sem=recv_sem.at[item],
                device_id={axis: peer},
                device_id_type=MESH,
            ).start()
            return carry

        lax.fori_loop(1, groups, send, 0)
    kept = []
    for item in range(count):
        dim = dims[item]
        source = ins[item] if dim is None else block(ins[item], dim, me)
        kept.append(
            pltpu.make_async_copy(source, block(outs[item], dim or 0, me), local_sem.at[item])
        )
        kept[-1].start()
    for item in range(count):
        kept[item].wait()
        rest = block(outs[item], dims[item] or 0, pl.ds(0, groups - 1))
        pltpu.make_async_copy(rest, rest, recv_sem.at[item]).wait()
        pltpu.make_async_copy(rest, rest, send_sem.at[item]).wait()


def push(arrays, dims, axis, ident):
    groups = lax.axis_size(axis)
    shapes = [
        jax.ShapeDtypeStruct((groups,) + a.shape if d is None else a.shape, a.dtype)
        for a, d in zip(arrays, dims)
    ]
    count = len(arrays)
    return pl.pallas_call(
        functools.partial(push_kernel, axis, groups, tuple(dims)),
        out_shape=shapes,
        in_specs=[pl.BlockSpec(memory_space=pltpu.VMEM)] * count,
        out_specs=[pl.BlockSpec(memory_space=pltpu.VMEM)] * count,
        scratch_shapes=[
            pltpu.SemaphoreType.DMA((count,)),
            pltpu.SemaphoreType.DMA((count,)),
            pltpu.SemaphoreType.DMA((count,)),
        ],
        compiler_params=pltpu.CompilerParams(
            collective_id=ident, has_side_effects=True, vmem_limit_bytes=48 * 1024 * 1024
        ),
        name=f"push{ident}",
    )(*arrays)


def shards(
    bag_lengths,
    owners,
    row_slots,
    admit_mask,
    expired,
    embeddings,
    accumulator,
    hidden_weight,
    output_weight,
    labels,
):
    groups = lax.axis_size("dp")
    halves = lax.axis_size("mp")
    tab_dev, tok_dev, bag_size = row_slots.shape
    rows_dev = embeddings.shape[1]
    row_width = embeddings.shape[2]
    lookups = tok_dev * bag_size
    capacity = 2 * lookups // groups
    buffer_len = groups * capacity
    f32, bf16, i32 = jnp.float32, jnp.bfloat16, jnp.int32

    places = jnp.arange(bag_size, dtype=i32)
    live = (places[None, None, :] < bag_lengths[:, :, None]) & (admit_mask == 1)
    counted = jnp.sum(live.astype(f32), axis=2)
    scale = 1.0 / jnp.maximum(counted, 1.0)

    target = owners[..., 0].reshape(tab_dev, lookups)
    flat_slots = row_slots.reshape(tab_dev, lookups)
    lookup_ids = jnp.arange(lookups, dtype=i32)
    sample_of = jnp.where(live.reshape(tab_dev, lookups), lookup_ids[None] // bag_size + 1, 0)
    owner_hot = (target[:, None, :] == jnp.arange(groups, dtype=i32)[None, :, None]).astype(bf16)
    earlier = (lookup_ids[:, None] < lookup_ids[None, :]).astype(bf16)
    running = jnp.dot(
        owner_hot.reshape(tab_dev * groups, lookups), earlier, preferred_element_type=f32
    ).reshape(tab_dev, groups, lookups)
    ranked = jnp.sum(jnp.where(owner_hot > 0, running, 0.0), axis=1).astype(i32)
    rank_hot = (ranked[:, None, :] == jnp.arange(capacity, dtype=i32)[None, :, None]).astype(bf16)
    digits = jnp.stack(
        [flat_slots // BASE, flat_slots % BASE, sample_of // BASE, sample_of % BASE], axis=1
    ).astype(bf16)
    coded = (digits[:, :, None, :] * owner_hot[:, None, :, :]).reshape(
        tab_dev, 4 * groups, lookups
    )
    table_of = jnp.einsum("tal,tkl->tak", coded, rank_hot, preferred_element_type=f32).astype(i32)
    table_of = table_of.reshape(tab_dev, 4, groups, capacity)
    request = table_of[:, 0] * BASE + table_of[:, 1]
    slot_sample = (table_of[:, 2] * BASE + table_of[:, 3]).reshape(tab_dev, buffer_len)

    (arrived,) = push([request.transpose(1, 0, 2)], [0], "dp", 0)
    arrived = arrived.transpose(1, 0, 2).reshape(tab_dev, buffer_len)
    fresh_rows = jnp.where(expired[:, :, None] == 1, f32(0.0), embeddings)
    fresh_acc = jnp.where(expired == 1, f32(ACC_RESET), accumulator)
    row_pick = (arrived[:, :, None] == jnp.arange(rows_dev, dtype=i32)[None, None, :]).astype(bf16)
    fetched = jnp.einsum(
        "tbr,tre->tbe", row_pick, fresh_rows.astype(bf16), preferred_element_type=f32
    ).astype(bf16)
    (returned,) = push(
        [fetched.reshape(tab_dev, groups, capacity, row_width)], [1], "dp", 1
    )
    returned = returned.reshape(tab_dev, buffer_len, row_width)
    sample_ids = jnp.arange(1, tok_dev + 1, dtype=i32)
    pool = (slot_sample[:, None, :] == sample_ids[None, :, None]).astype(bf16)
    pooled = jnp.einsum("tnb,tbe->tne", pool, returned, preferred_element_type=f32)
    pooled = (pooled * scale[:, :, None]).astype(bf16)
    features = pooled.transpose(1, 0, 2).reshape(tok_dev, tab_dev * row_width)
    portion = lax.all_gather(features, "mp", axis=1, tiled=True)
    summed_pre = jnp.dot(portion, hidden_weight, preferred_element_type=f32)
    hidden = jax.nn.silu(summed_pre).astype(bf16)
    logits = lax.psum(jnp.sum(hidden.astype(f32) * output_weight, axis=1), "mp")
    dlogit = jax.nn.sigmoid(logits) - labels.astype(f32)
    dhidden = (dlogit[:, None] * output_weight * silu_slope(summed_pre)).astype(bf16)
    partial = lax.dot_general(
        dhidden, hidden_weight, (((1,), (1,)), ((), ())), preferred_element_type=f32
    ).astype(bf16)
    partial = partial.reshape(tok_dev, halves, tab_dev * row_width).transpose(1, 0, 2)
    (both,) = push([partial], [0], "mp", 2)
    feature_grad = jnp.sum(both.astype(f32), axis=0)
    per_table = feature_grad.reshape(tok_dev, tab_dev, row_width).transpose(1, 0, 2)
    per_table = (per_table * scale[:, :, None]).astype(bf16)
    sample_pick = (slot_sample[:, :, None] == sample_ids[None, None, :]).astype(bf16)
    outgoing = jnp.einsum(
        "tbn,tne->tbe", sample_pick, per_table, preferred_element_type=f32
    ).astype(bf16)
    share = portion.shape[1] // groups
    columns = portion.T.reshape(groups, share, tok_dev)
    grad_part, all_dhidden, all_columns = push(
        [outgoing.reshape(tab_dev, groups, capacity, row_width), dhidden, columns],
        [1, None, 0],
        "dp",
        3,
    )
    dense = jnp.einsum("gfn,gnh->fh", all_columns, all_dhidden, preferred_element_type=f32)
    (weight_grad,) = push([dense.astype(bf16)], [None], "dp", 4)
    weight_grad = weight_grad.reshape(portion.shape[1], dhidden.shape[1])
    selector = (arrived[:, None, :] == jnp.arange(rows_dev, dtype=i32)[None, :, None]).astype(bf16)
    summed = jnp.einsum(
        "trb,tbe->tre",
        selector,
        grad_part.reshape(tab_dev, buffer_len, row_width),
        preferred_element_type=f32,
    )
    new_acc = fresh_acc + jnp.mean(summed * summed, axis=2)
    new_rows = fresh_rows - LEARN_RATE * summed / jnp.sqrt(new_acc)[:, :, None]
    return (new_rows, new_acc, weight_grad, logits)


def solution(mesh):
    in_specs = (
        P("mp", "dp"),
        P("mp", "dp", None, None),
        P("mp", "dp", None),
        P("mp", "dp", None),
        P("mp", "dp"),
        P("mp", "dp", None),
        P("mp", "dp"),
        P(None, "mp"),
        P("mp"),
        P("dp"),
    )
    out_specs = (P("mp", "dp", None), P("mp", "dp"), P(None, "mp"), P("dp"))
    return jax.shard_map(shards, mesh=mesh, in_specs=in_specs, out_specs=out_specs, check_vma=False)
```

time: 404 us -> 379 us (0.938); the launches traced: 399 us -> 379 us
  Pallas kernels: 0 us -> 315 us
  waiting for transfers between devices: 184 us -> 0 us
  other arithmetic: 86.1 us -> 4.59 us
  local copies, waits for them, and re-layouts: 46.8 us -> 14.2 us
  starting transfers between devices: 20.7 us -> 0 us
  between operations: 13.9 us -> 0.91 us
  matrix products: 36.1 us -> 32 us
    pallas_call x0 -> x5, Pallas kernels: none -> 315 us  [push(): pl.pallas_call(functools.partial(push_kernel, axis, groups, tuple(dims)),...]
    reduce_scatter x2 -> x0, waiting for transfers between devices: 108 us -> none  [the longest x1 106 us: shards(): lax.psum_scatter(local_grad, 'dp', scatter_dimension=0, tiled=True)]
    reduce_sum x5 -> x2, other arithmetic: 78.7 us -> 0.87 us  [the longest x1 0.78 us: shards(): counted = jnp.sum(live.astype(f32), axis=2)]
    all_to_all x3 -> x0, waiting for transfers between devices: 73.6 us -> none  [the longest x1 61.9 us: shards(): lax.all_to_all(fetched, 'dp', split_axis=1, concat_axis=1, tiled=True)]
    all_to_all x3 -> x0, starting transfers between devices: 20.2 us -> none  [the longest x1 7.16 us: shards(): lax.all_to_all(fetched, 'dp', split_axis=1, concat_axis=1, tiled=True)]
    reshape x5 -> x3, local copies, waits for them, and re-layouts: 20.3 us -> 1.87 us  [the longest x1 1.24 us: shards(): partial.reshape(tok_dev, halves, tab_dev * row_width).transpose(1, 0, 2)]
    all_to_all x2 -> x0, local copies, waits for them, and re-layouts: 13.6 us -> none  [the longest x1 6.83 us: shards(): lax.all_to_all(fetched, 'dp', split_axis=1, concat_axis=1, tiled=True)]
    dot_general x7 -> x9, matrix products: 36.1 us -> 32 us  [the longest x1 9.81 us: shards(): jnp.einsum('trb,tbe->tre', selector, grad_part.reshape(tab_dev, buffer_le...]
  transfers between devices with their start and end apart: 6 -> 0, of which waited for: 6 -> 0; matrix products, arithmetic and copies ran while one was open for 21% -> 0% of each run, Pallas kernels for 0% -> 0%
where the time goes in v1:
time: 379 us
  Pallas kernels  315 us (83%)
  matrix products  32 us (8%)
  local copies, waits for them, and re-layouts  14.2 us (4%)
  blocking collectives  11.9 us (3%)
  other arithmetic  4.59 us (1%)
    pallas_call x5, Pallas kernels, push(): pl.pallas_call(functools.partial(push_kernel, axis, groups, tuple(dims)),...  315 us
    dot_general x1, matrix products, shards(): jnp.einsum('trb,tbe->tre', selector, grad_part.reshape(tab_dev, buffer_le...  9.81 us
    unnamed x23, local copies, waits for them, and re-layouts  9.6 us
    dot_general x1, matrix products, shards(): jnp.einsum('tbr,tre->tbe', row_pick, fresh_rows.astype(bf16), preferred_e...  8.69 us
    all_gather x1, blocking collectives, shards(): portion = lax.all_gather(features, 'mp', axis=1, tiled=True)  7.93 us

profile of v1, /device:TPU:15, one launch (start us, length us, event | category | flops | bytes accessed | tf_op | source)
XLA Modules:
  0.0 378.7 jit_solution(14276359980478122013)
XLA Ops:
  0.6 0.0 copy-start
  0.7 0.9 broadcast_compare_fusion
  1.5 0.8 convert_reduce_fusion.1
  2.3 0.3 copy.35
  2.6 0.0 copy-start.4
  2.6 0.4 reshape.407
  3.0 1.0 copy.37
  3.9 0.3 eq.110
  4.2 0.5 fusion.33
  4.8 0.0 copy-done.4
  4.8 0.2 copy.34
  5.0 0.3 reshape.406
  5.2 0.1 fusion.47
  5.3 0.1 copy.36
  5.4 0.1 broadcast_multiply_fusion
  5.5 0.9 fusion.36
  6.4 0.2 copy.38
  6.6 7.0 %push0.1 = s32[16,8,128]{2,1,0:T(8,128)S(1)} custom-call(s32[16,8,128]{2,1,0:T(8,128)S(1)} %get-tuple-element.26.refs_0_), custom_call_target="tpu_custom_call" | custom-call | tf_op jit(solution)/shard_map/push0/pallas_call | solution.py:79
  13.6 2.9 copy.33
  16.5 8.7 %fusion.19 = bf16[8,2048,128]{2,1,0:T(8,128)(2,1)} fusion(s32[8,2048]{1,0:T(8,128)S(1)} %bitcast.61, f32[8,512,128]{1,2,0:T(8,128)} %copy.33, pred[8,512]{1,0:T(8,128)(4,1)S(1)} %broadcast_compare_fusion), kind=kOutput, calls=%fused_computation.20 | convolution fusion | flops 2158493696 | bytes 6361088 | tf_op jit(solution)/shard_map/tbr,tre->tbe/dot_general | solution.py:150
  25.1 97.0 %push1.1 = bf16[8,16,128,128]{3,2,1,0:T(8,128)(2,1)S(1)} custom-call(bf16[8,16,128,128]{3,2,1,0:T(8,128)(2,1)} %bitcast.64), custom_call_target="tpu_custom_call" | custom-call | tf_op jit(solution)/shard_map/push1/pallas_call | solution.py:79
  122.1 0.0 copy-start.6
  122.2 2.1 fusion.30
  124.3 0.0 copy-start.7
  124.3 7.9 %all_gather.3 = bf16[128,2048]{0,1:T(8,128)(2,1)S(1)} all-gather(bf16[128,1024]{0,1:T(8,128)(2,1)S(1)} %bitcast.69), channel_id=1, replica_groups=mesh['dp'=16,'mp'=2] {'mp'}, dimensions={1}, use_global_device_ids=true | all-gather | bytes 786432 | tf_op jit(solution)/shard_map/all_gather | solution.py:162
  132.2 0.0 copy-done
  132.2 0.0 copy-done.6
  132.2 0.6 multiply_reduce_fusion.1
  132.8 4.0 %psum.7 = f32[128]{0:T(128)S(1)} all-reduce(f32[128]{0:T(128)S(1)} %get-tuple-element.34), channel_id=1, replica_groups=mesh['dp'=16,'mp'=2] {'mp'}, use_global_device_ids=true, to_apply=%region_3.4 | all-reduce | flops 128 | bytes 1024 | tf_op jit(solution)/shard_map/psum | solution.py:165
  136.8 0.0 copy-done.7
  136.8 0.0 copy-start.8
  136.8 0.1 multiply_convert_fusion.2.refs_1_
  136.9 0.8 convolution_convert_fusion
  137.8 1.0 copy.41
  138.8 0.0 copy-done.8
  138.8 1.2 copy.42
  140.0 6.8 %push2.1 = bf16[2,128,1024]{2,1,0:T(8,128)(2,1)S(1)} custom-call(bf16[2,128,1024]{2,1,0:T(8,128)(2,1)S(1)} %bitcast.60), custom_call_target="tpu_custom_call" | custom-call | tf_op jit(solution)/shard_map/push2/pallas_call | solution.py:79
  146.9 0.1 convert_reduce_fusion
  147.0 1.0 copy.43
  148.0 6.6 %fusion.16 = bf16[8,2048,128]{2,1,0:T(8,128)(2,1)} fusion(s32[128]{0:T(128)S(1)} %iota_add_fusion, s32[8,2048]{1,0:T(8,128)S(1)} %get-tuple-element.27, f32[8,128,128]{1,2,0:T(8,128)} %bitcast.68, f32[8,128]{1,0:T(8,128)S(1)} %get-tuple-element.32), kind=kOutput, calls=%fused_computation.19 | convolution fusion | flops 541327360 | bytes 4788736 | tf_op jit(solution)/shard_map/tbn,tne->tbe/dot_general | solution.py:177
  154.6 155.5 %push3.1 = (bf16[8,16,128,128]{3,2,1,0:T(8,128)(2,1)}, bf16[16,128,512]{2,1,0:T(8,128)(2,1)S(1)}, bf16[16,128,128]{2,1,0:T(8,128)(2,1)S(1)}) custom-call(bf16[8,16,128,128]{3,2,1,0:T(8,128)(2,1)} %bitcast.63, bf16[128,512]{1,0:T(8,128)(2,1)S(1)} %multiply_convert_fusion.2.refs_1_, bf16[16,128,128]{2,1,0:T(8,128)(2,1)S(1)} %bitcast.59), custom_call_target="tpu_custom_call" | custom-call | tf_op jit(solution)/shard_map/push3/pallas_call | solution.py:79
  310.1 0.0 copy-start.1
  310.1 1.3 copy-done.1
  311.5 0.0 copy-start.3
  311.5 0.0 copy-start.5
  311.5 0.0 copy-start.2
  311.5 9.8 %multiply_reduce_fusion = (f32[8,512]{1,0:T(8,128)S(1)}, f32[8,512,128]{1,2,0:T(8,128)S(1)}) fusion(bf16[8,2048,128]{2,1,0:T(8,128)(2,1)} %bitcast.70, s32[8,2048]{1,0:T(8,128)S(1)} %bitcast.62), kind=kOutput, calls=%fused_computation.23 | convolution fusion | flops 2156916736 | bytes 6373376 | tf_op jit(solution)/shard_map/trb,tbe->tre/dot_general | solution.py:192
  321.3 0.0 copy-done.3
  321.3 0.0 copy-done.5
  321.3 0.6 fusion.63
  321.9 0.0 copy-done.2
  321.9 1.8 divide_subtract_fusion
  323.8 2.9 copy.46
  326.6 2.0 fusion.37.refs_0_
  328.7 48.7 %push4.1 = bf16[16,128,512]{2,1,0:T(8,128)(2,1)S(1)} custom-call(bf16[128,512]{1,0:T(8,128)(2,1)S(1)} %fusion.37.refs_0_), custom_call_target="tpu_custom_call" | custom-call | tf_op jit(solution)/shard_map/push4/pallas_call | solution.py:79
  377.3 1.3 copy.52
  (8 shorter events, 0.1 us)
Async XLA Ops:
  0.6 131.6 %copy-start = (bf16[2048,512]{1,0:T(8,128)(2,1)S(1)}, bf16[2048,512]{1,0:T(8,128)(2,1)}, u32[]{:S(2)}) copy-start(bf16[2048,512]{1,0:T(8,128)(2,1)} %param.17) | copy-start | bytes 6291460
  2.6 2.2 copy-start.4
  122.1 10.1 %copy-start.6 = (f32[512]{0:T(512)S(1)}, f32[512]{0:T(512)}, u32[]{:S(2)}) copy-start(f32[512]{0:T(512)} %param.18) | copy-start | bytes 6148
  124.3 12.5 %copy-start.7 = (s32[128]{0:T(128)S(1)}, s32[128]{0:T(128)}, u32[]{:S(2)}) copy-start(s32[128]{0:T(128)} %param.19) | copy-start | bytes 1540
  136.8 2.0 copy-start.8
  310.1 1.3 copy-start.1
  311.5 9.8 %copy-start.3 = (s32[8,512]{1,0:T(8,128)S(1)}, s32[8,512]{1,0:T(8,128)}, u32[]{:S(2)}) copy-start(s32[8,512]{1,0:T(8,128)} %param.14) | copy-start | bytes 49156
  311.5 9.8 %copy-start.5 = (f32[8,512]{1,0:T(8,128)S(1)}, f32[8,512]{1,0:T(8,128)}, u32[]{:S(2)}) copy-start(f32[8,512]{1,0:T(8,128)} %param.16) | copy-start | bytes 49156
  311.5 10.5 %copy-start.2 = (f32[8,512,128]{1,2,0:T(8,128)S(1)}, f32[8,512,128]{1,2,0:T(8,128)}, u32[]{:S(2)}) copy-start(f32[8,512,128]{1,2,0:T(8,128)} %copy.33) | copy-start | bytes 6291460

commit v2 on v1

--- a/solution.py
+++ b/solution.py
@@ -90,6 +90,131 @@
             collective_id=ident, has_side_effects=True, vmem_limit_bytes=48 * 1024 * 1024
         ),
         name=f"push{ident}",
+    )(*arrays)
+
+
+def grid_of(groups):
+    chips = groups // 2
+    inner = 1
+    while inner * inner * 4 <= chips and chips % (inner * 2) == 0:
+        inner *= 2
+    return chips // inner, inner
+
+
+def gather_kernel(axis, groups, count, *refs):
+    ins, outs = refs[:count], refs[count : 2 * count]
+    send_sem, outer_sem, inner_sem, core_sem, local_sem = refs[2 * count :]
+    outer, inner = grid_of(groups)
+    me = lax.axis_index(axis)
+    core = lax.rem(me, 2)
+    row = lax.rem(lax.div(me, 2), inner)
+    plane = lax.div(me, 2 * inner)
+    partner = me + 1 - 2 * core
+
+    def device(p, r):
+        return (p * inner + r) * 2 + core
+
+    def plane_peer(step):
+        return device(lax.rem(plane + step, outer), row)
+
+    def row_peer(step):
+        return device(plane, lax.rem(row + step, inner))
+
+    def source(up, across):
+        return device(lax.rem(plane + outer - up, outer), lax.rem(row + inner - across, inner))
+
+    barrier = pltpu.get_barrier_semaphore()
+
+    def greet(peer):
+        pl.semaphore_signal(barrier, inc=1, device_id={axis: peer}, device_id_type=MESH)
+
+    def loop(low, high, body):
+        def step(index, carry):
+            body(index)
+            return carry
+
+        lax.fori_loop(low, high, step, 0)
+
+    loop(1, outer, lambda step: greet(plane_peer(step)))
+    loop(1, inner, lambda step: greet(row_peer(step)))
+    greet(partner)
+    pl.semaphore_wait(barrier, outer + inner - 1)
+
+    def send(item, src, owner, sem, peer):
+        pltpu.make_async_remote_copy(
+            src_ref=src,
+            dst_ref=outs[item].at[owner],
+            send_sem=send_sem.at[item],
+            recv_sem=sem,
+            device_id={axis: peer},
+            device_id_type=MESH,
+        ).start()
+
+    def spread(item, src, owner, up):
+        loop(
+            1,
+            inner,
+            lambda step: send(item, src, owner, inner_sem.at[item, up, step], row_peer(step)),
+        )
+        send(item, src, owner, core_sem.at[item], partner)
+
+    def arrive(item, owner, sem):
+        pltpu.make_async_copy(outs[item].at[owner], outs[item].at[owner], sem).wait()
+
+    for item in range(count):
+        loop(
+            1,
+            outer,
+            lambda step: send(item, ins[item], me, outer_sem.at[item, step], plane_peer(step)),
+        )
+        spread(item, ins[item], me, 0)
+    kept = []
+    for item in range(count):
+        kept.append(pltpu.make_async_copy(ins[item], outs[item].at[me], local_sem.at[item]))
+        kept[-1].start()
+
+    def from_plane(item, up):
+        owner = source(up, 0)
+        arrive(item, owner, outer_sem.at[item, up])
+        spread(item, outs[item].at[owner], owner, up)
+
+    def from_row(item, up, across):
+        owner = source(up, across)
+        arrive(item, owner, inner_sem.at[item, up, across])
+        send(item, outs[item].at[owner], owner, core_sem.at[item], partner)
+
+    for item in range(count):
+        loop(1, outer, lambda up: from_plane(item, up))
+    for item in range(count):
+        loop(0, outer, lambda up: loop(1, inner, lambda across: from_row(item, up, across)))
+    for item in range(count):
+        kept[item].wait()
+        part = outs[item].at[pl.ds(0, outer * inner)]
+        pltpu.make_async_copy(part, part, core_sem.at[item]).wait()
+        rest = outs[item].at[pl.ds(0, groups - 1)]
+        pltpu.make_async_copy(rest, rest, send_sem.at[item]).wait()
+
+
+def gather(arrays, axis, ident):
+    groups = lax.axis_size(axis)
+    outer, inner = grid_of(groups)
+    count = len(arrays)
+    return pl.pallas_call(
+        functools.partial(gather_kernel, axis, groups, count),
+        out_shape=[jax.ShapeDtypeStruct((groups,) + a.shape, a.dtype) for a in arrays],
+        in_specs=[pl.BlockSpec(memory_space=pltpu.VMEM)] * count,
+        out_specs=[pl.BlockSpec(memory_space=pltpu.VMEM)] * count,
+        scratch_shapes=[
+            pltpu.SemaphoreType.DMA((count,)),
+            pltpu.SemaphoreType.DMA((count, outer)),
+            pltpu.SemaphoreType.DMA((count, outer, inner)),
+            pltpu.SemaphoreType.DMA((count,)),
+            pltpu.SemaphoreType.DMA((count,)),
+        ],
+        compiler_params=pltpu.CompilerParams(
+            collective_id=ident, has_side_effects=True, vmem_limit_bytes=48 * 1024 * 1024
+        ),
+        name=f"gather{ident}",
     )(*arrays)
 
 
@@ -142,8 +267,11 @@
     request = table_of[:, 0] * BASE + table_of[:, 1]
     slot_sample = (table_of[:, 2] * BASE + table_of[:, 3]).reshape(tab_dev, buffer_len)
 
-    (arrived,) = push([request.transpose(1, 0, 2)], [0], "dp", 0)
-    arrived = arrived.transpose(1, 0, 2).reshape(tab_dev, buffer_len)
+    packed = request * (tok_dev + 1) + slot_sample.reshape(tab_dev, groups, capacity)
+    (arrived,) = push([packed.transpose(1, 0, 2)], [0], "dp", 0)
+    arrived = arrived.transpose(1, 0, 2)
+    came_from = arrived % (tok_dev + 1)
+    arrived = (arrived // (tok_dev + 1)).reshape(tab_dev, buffer_len)
     fresh_rows = jnp.where(expired[:, :, None] == 1, f32(0.0), embeddings)
     fresh_acc = jnp.where(expired == 1, f32(ACC_RESET), accumulator)
     row_pick = (arrived[:, :, None] == jnp.arange(rows_dev, dtype=i32)[None, None, :]).astype(bf16)
@@ -173,20 +301,16 @@
     feature_grad = jnp.sum(both.astype(f32), axis=0)
     per_table = feature_grad.reshape(tok_dev, tab_dev, row_width).transpose(1, 0, 2)
     per_table = (per_table * scale[:, :, None]).astype(bf16)
-    sample_pick = (slot_sample[:, :, None] == sample_ids[None, None, :]).astype(bf16)
-    outgoing = jnp.einsum(
-        "tbn,tne->tbe", sample_pick, per_table, preferred_element_type=f32
-    ).astype(bf16)
     share = portion.shape[1] // groups
     columns = portion.T.reshape(groups, share, tok_dev)
-    grad_part, all_dhidden, all_columns = push(
-        [outgoing.reshape(tab_dev, groups, capacity, row_width), dhidden, columns],
-        [1, None, 0],
-        "dp",
-        3,
-    )
+    (all_columns,) = push([columns], [0], "dp", 3)
+    all_dhidden, all_grads = gather([dhidden, per_table], "dp", 5)
+    sample_pick = (came_from[..., None] == sample_ids).astype(bf16)
+    grad_part = jnp.einsum(
+        "tgkn,gtne->tgke", sample_pick, all_grads, preferred_element_type=f32
+    ).astype(bf16)
     dense = jnp.einsum("gfn,gnh->fh", all_columns, all_dhidden, preferred_element_type=f32)
-    (weight_grad,) = push([dense.astype(bf16)], [None], "dp", 4)
+    (weight_grad,) = gather([dense.astype(bf16)], "dp", 4)
     weight_grad = weight_grad.reshape(portion.shape[1], dhidden.shape[1])
     selector = (arrived[:, None, :] == jnp.arange(rows_dev, dtype=i32)[None, :, None]).astype(bf16)
     summed = jnp.einsum(

time: 379 us -> 265 us (0.70)
  Pallas kernels: 315 us -> 201 us
    pallas_call x5 -> x4, Pallas kernels: 315 us -> 127 us  [push(): pl.pallas_call(functools.partial(push_kernel, axis, groups, tuple(dims)),...]
    pallas_call x0 -> x2, Pallas kernels: none -> 73.7 us  [gather(): pl.pallas_call(functools.partial(gather_kernel, axis, groups, count), out...]
    unnamed x23 -> x21, local copies, waits for them, and re-layouts: 9.6 us -> 8.27 us
where the time goes in v2:
time: 265 us; the launch traced here: 263 us
  Pallas kernels  201 us (76%)
  matrix products  29.9 us (11%)
  local copies, waits for them, and re-layouts  14.1 us (5%)
  blocking collectives  11.9 us (4%)
  other arithmetic  4.86 us (2%)
    pallas_call x4, Pallas kernels, push(): pl.pallas_call(functools.partial(push_kernel, axis, groups, tuple(dims)),...  127 us
    pallas_call x2, Pallas kernels, gather(): pl.pallas_call(functools.partial(gather_kernel, axis, groups, count), out...  73.7 us
    dot_general x1, matrix products, shards(): jnp.einsum('trb,tbe->tre', selector, grad_part.reshape(tab_dev, buffer_le...  9.81 us
    dot_general x1, matrix products, shards(): jnp.einsum('tbr,tre->tbe', row_pick, fresh_rows.astype(bf16), preferred_e...  8.7 us
    unnamed x21, local copies, waits for them, and re-layouts  8.27 us
    all_gather x1, blocking collectives, shards(): portion = lax.all_gather(features, 'mp', axis=1, tiled=True)  7.93 us
    dot_general x1, matrix products, shards(): jnp.einsum('tgkn,gtne->tgke', sample_pick, all_grads, preferred_element_t...  6.11 us

profile of v2, /device:TPU:15, one launch (start us, length us, event | category | flops | bytes accessed | tf_op | source)
XLA Modules:
  0.0 262.8 jit_solution(10743810566312814436)
XLA Ops:
  0.6 0.0 copy-start
  0.7 0.9 broadcast_compare_fusion
  1.5 0.8 convert_reduce_fusion.1
  2.3 0.3 copy.39
  2.6 0.0 copy-start.3
  2.6 0.4 reshape.401
  3.0 1.0 copy.41
  3.9 0.3 eq.112
  4.2 0.5 fusion.36
  4.8 0.0 copy-done.3
  4.8 0.2 copy.38
  5.0 0.3 reshape.400
  5.2 0.1 fusion.55
  5.3 0.1 copy.40
  5.4 0.1 broadcast_multiply_fusion
  5.5 0.9 fusion.39
  6.4 0.2 copy.42
  6.6 7.0 %push0.1 = s32[16,8,128]{2,1,0:T(8,128)S(1)} custom-call(s32[16,8,128]{2,1,0:T(8,128)S(1)} %get-tuple-element.25.refs_0_), custom_call_target="tpu_custom_call" | custom-call | tf_op jit(solution)/shard_map/push0/pallas_call | solution.py:79
  13.6 0.1 add_select_fusion
  13.7 2.9 %copy.37 = f32[8,512,128]{1,2,0:T(8,128)} copy(f32[8,512,128]{2,1,0:T(8,128)} %param.15) | data formatting | bytes 4194304 | tf_op args[5]
  16.6 8.7 %fusion.17 = bf16[8,2048,128]{2,1,0:T(8,128)(2,1)} fusion(s32[8,2048]{1,0:T(8,128)S(1)} %get-tuple-element.27, f32[8,512,128]{1,2,0:T(8,128)} %copy.37, pred[8,512]{1,0:T(8,128)(4,1)S(1)} %broadcast_compare_fusion), kind=kOutput, calls=%fused_computation.20 | convolution fusion | flops 2158493696 | bytes 6361088 | tf_op jit(solution)/shard_map/tbr,tre->tbe/dot_general | solution.py:278
  25.2 97.0 %push1.1 = bf16[8,16,128,128]{3,2,1,0:T(8,128)(2,1)S(1)} custom-call(bf16[8,16,128,128]{3,2,1,0:T(8,128)(2,1)} %bitcast.81), custom_call_target="tpu_custom_call" | custom-call | tf_op jit(solution)/shard_map/push1/pallas_call | solution.py:79
  122.2 0.0 copy-start.5
  122.3 2.1 fusion.33
  124.4 0.0 copy-start.6
  124.4 7.9 %all_gather.3 = bf16[128,2048]{0,1:T(8,128)(2,1)S(1)} all-gather(bf16[128,1024]{0,1:T(8,128)(2,1)S(1)} %bitcast.86), channel_id=1, replica_groups=mesh['dp'=16,'mp'=2] {'mp'}, dimensions={1}, use_global_device_ids=true | all-gather | bytes 786432 | tf_op jit(solution)/shard_map/all_gather | solution.py:290
  132.3 0.0 copy-done
  132.3 0.0 copy-done.5
  132.3 0.6 multiply_reduce_fusion.1
  132.9 4.0 %psum.7 = f32[128]{0:T(128)S(1)} all-reduce(f32[128]{0:T(128)S(1)} %get-tuple-element.34), channel_id=1, replica_groups=mesh['dp'=16,'mp'=2] {'mp'}, use_global_device_ids=true, to_apply=%region_3.4 | all-reduce | flops 128 | bytes 1024 | tf_op jit(solution)/shard_map/psum | solution.py:293
  136.9 0.0 copy-done.6
  136.9 0.0 copy-start.7
  136.9 0.1 multiply_convert_fusion.refs_0_
  137.1 0.8 convolution_convert_fusion
  137.9 1.0 copy.46
  138.9 0.0 copy-done.7
  138.9 1.2 copy.47
  140.1 6.8 %push2.1 = bf16[2,128,1024]{2,1,0:T(8,128)(2,1)S(1)} custom-call(bf16[2,128,1024]{2,1,0:T(8,128)(2,1)S(1)} %bitcast.80), custom_call_target="tpu_custom_call" | custom-call | tf_op jit(solution)/shard_map/push2/pallas_call | solution.py:79
  147.0 0.1 convert_reduce_fusion
  147.1 1.0 copy.48
  148.1 1.2 copy.49
  149.3 0.2 fusion.43.refs_1_
  149.5 16.5 %push3.1 = bf16[16,128,128]{2,1,0:T(8,128)(2,1)S(1)} custom-call(bf16[16,128,128]{2,1,0:T(8,128)(2,1)S(1)} %bitcast.79), custom_call_target="tpu_custom_call" | custom-call | tf_op jit(solution)/shard_map/push3/pallas_call | solution.py:79
  166.0 48.7 %gather5.1 = (bf16[16,128,512]{2,1,0:T(8,128)(2,1)S(1)}, bf16[16,8,128,128]{3,2,1,0:T(8,128)(2,1)}) custom-call(bf16[128,512]{1,0:T(8,128)(2,1)S(1)} %multiply_convert_fusion.refs_0_, bf16[8,128,128]{2,1,0:T(8,128)(2,1)S(1)} %fusion.43.refs_1_), custom_call_target="tpu_custom_call" | custom-call | tf_op jit(solution)/shard_map/gather5/pallas_call | solution.py:202
  214.7 0.4 fusion.40.refs_0_
  215.1 6.1 %fusion.18 = bf16[8,16,128,128]{3,2,1,0:T(8,128)(2,1)} fusion(bf16[16,8,128,128]{3,2,1,0:T(8,128)(2,1)} %get-tuple-element.6, s32[128]{0:T(128)S(1)} %iota_add_fusion, s32[8,16,128]{2,1,0:T(8,128)S(1)} %copy.43), kind=kOutput, calls=%fused_computation.21 | convolution fusion | flops 541065216 | bytes 8454656 | tf_op jit(solution)/shard_map/tgkn,gtne->tgke/dot_general | solution.py:309
  221.2 0.0 copy-start.2
  221.2 0.0 copy-start.4
  221.2 0.0 copy-start.1
  221.3 9.8 %multiply_reduce_fusion = (f32[8,512]{1,0:T(8,128)S(1)}, f32[8,512,128]{1,2,0:T(8,128)S(1)}) fusion(bf16[8,2048,128]{2,1,0:T(8,128)(2,1)} %bitcast.87, s32[8,2048]{1,0:T(8,128)S(1)} %get-tuple-element.27), kind=kOutput, calls=%fused_computation.24 | convolution fusion | flops 2156916736 | bytes 6373376 | tf_op jit(solution)/shard_map/trb,tbe->tre/dot_general | solution.py:316
  231.1 0.0 copy-done.2
  231.1 0.0 copy-done.4
  231.1 0.6 fusion.72
  231.7 0.0 copy-done.1
  231.7 1.8 divide_subtract_fusion
  233.6 2.9 %copy.52 = f32[8,512,128]{2,1,0:T(8,128)} copy(f32[8,512,128]{1,2,0:T(8,128)} %divide_subtract_fusion) | data formatting | bytes 4194304
  236.4 25.0 %gather4.1 = bf16[16,128,512]{2,1,0:T(8,128)(2,1)S(1)} custom-call(bf16[128,512]{1,0:T(8,128)(2,1)S(1)} %fusion.40.refs_0_), custom_call_target="tpu_custom_call" | custom-call | tf_op jit(solution)/shard_map/gather4/pallas_call | solution.py:202
  261.4 1.3 copy.61
  (9 shorter events, 0.1 us)
Async XLA Ops:
  0.6 131.7 %copy-start = (bf16[2048,512]{1,0:T(8,128)(2,1)S(1)}, bf16[2048,512]{1,0:T(8,128)(2,1)}, u32[]{:S(2)}) copy-start(bf16[2048,512]{1,0:T(8,128)(2,1)} %param.17) | copy-start | bytes 6291460
  2.6 2.2 copy-start.3
  122.2 10.1 %copy-start.5 = (f32[512]{0:T(512)S(1)}, f32[512]{0:T(512)}, u32[]{:S(2)}) copy-start(f32[512]{0:T(512)} %param.18) | copy-start | bytes 6148
  124.4 12.5 %copy-start.6 = (s32[128]{0:T(128)S(1)}, s32[128]{0:T(128)}, u32[]{:S(2)}) copy-start(s32[128]{0:T(128)} %param.19) | copy-start | bytes 1540
  136.9 2.0 copy-start.7
  221.2 9.8 %copy-start.2 = (s32[8,512]{1,0:T(8,128)S(1)}, s32[8,512]{1,0:T(8,128)}, u32[]{:S(2)}) copy-start(s32[8,512]{1,0:T(8,128)} %param.14) | copy-start | bytes 49156
  221.2 9.8 %copy-start.4 = (f32[8,512]{1,0:T(8,128)S(1)}, f32[8,512]{1,0:T(8,128)}, u32[]{:S(2)}) copy-start(f32[8,512]{1,0:T(8,128)} %param.16) | copy-start | bytes 49156
  221.2 10.5 %copy-start.1 = (f32[8,512,128]{1,2,0:T(8,128)S(1)}, f32[8,512,128]{1,2,0:T(8,128)}, u32[]{:S(2)}) copy-start(f32[8,512,128]{1,2,0:T(8,128)} %copy.37) | copy-start | bytes 6291460

commit v3 on v2

--- a/solution.py
+++ b/solution.py
@@ -40,8 +40,9 @@
     for item in range(count):
         dim = dims[item]
 
-        def send(step, carry, item=item, dim=dim):
-            peer = lax.rem(me + step, groups)
+        def send(turn, carry, item=item, dim=dim):
+            half, odd = lax.div(turn + 1, 2), lax.rem(turn, 2)
+            peer = lax.rem(me + odd * half + (1 - odd) * (groups - half), groups)
             source = ins[item] if dim is None else block(ins[item], dim, peer)
             pltpu.make_async_remote_copy(
                 src_ref=source,
@@ -303,7 +304,7 @@
     per_table = (per_table * scale[:, :, None]).astype(bf16)
     share = portion.shape[1] // groups
     columns = portion.T.reshape(groups, share, tok_dev)
-    (all_columns,) = push([columns], [0], "dp", 3)
+    all_columns = lax.all_to_all(columns, "dp", split_axis=0, concat_axis=0, tiled=True)
     all_dhidden, all_grads = gather([dhidden, per_table], "dp", 5)
     sample_pick = (came_from[..., None] == sample_ids).astype(bf16)
     grad_part = jnp.einsum(

time: 265 us -> 253 us (0.955)
  Pallas kernels: 201 us -> 181 us
  starting transfers between devices: 0 us -> 8.62 us
  matrix products: 29.9 us -> 33.6 us
  local copies, waits for them, and re-layouts: 14.1 us -> 10.7 us
    pallas_call x4 -> x3, Pallas kernels: 127 us -> 108 us  [push(): pl.pallas_call(functools.partial(push_kernel, axis, groups, tuple(dims)),...]
    all_to_all x0 -> x1, starting transfers between devices: none -> 8.62 us  [shards(): lax.all_to_all(columns, 'dp', split_axis=0, concat_axis=0, tiled=True)]
    unnamed x21 -> x27, local copies, waits for them, and re-layouts: 8.27 us -> 8.42 us
  transfers between devices with their start and end apart: 0 -> 1, of which waited for: 0 -> 0; matrix products, arithmetic and copies ran while one was open for 0% -> 10% of each run, Pallas kernels for 0% -> 22%
where the time goes in v3:
time: 253 us; the launch traced here: 251 us
  Pallas kernels  181 us (72%)
  matrix products  33.6 us (13%)
  blocking collectives  12 us (5%)
  local copies, waits for them, and re-layouts  10.7 us (4%)
  starting transfers between devices  8.62 us (3%)
  other arithmetic  3.25 us (1%)
    pallas_call x3, Pallas kernels, push(): pl.pallas_call(functools.partial(push_kernel, axis, groups, tuple(dims)),...  108 us
    pallas_call x2, Pallas kernels, gather(): pl.pallas_call(functools.partial(gather_kernel, axis, groups, count), out...  72.9 us
    dot_general x1, matrix products, shards(): jnp.einsum('trb,tbe->tre', selector, grad_part.reshape(tab_dev, buffer_le...  9.81 us
    dot_general x1, matrix products, shards(): jnp.einsum('tbr,tre->tbe', row_pick, fresh_rows.astype(bf16), preferred_e...  8.7 us
    all_to_all x1, starting transfers between devices, shards(): lax.all_to_all(columns, 'dp', split_axis=0, concat_axis=0, tiled=True)  8.62 us
    unnamed x27, local copies, waits for them, and re-layouts  8.42 us
    all_gather x1, blocking collectives, shards(): portion = lax.all_gather(features, 'mp', axis=1, tiled=True)  7.66 us
    dot_general x1, matrix products, shards(): jnp.einsum('tgkn,gtne->tgke', sample_pick, all_grads, preferred_element_t...  6.88 us
  transfers between devices with their start and end apart: 1, of which 0 were waited for; matrix products, arithmetic and copies ran while one was open for 10% of the time, Pallas kernels for 22%

profile of v3, /device:TPU:15, one launch (start us, length us, event | category | flops | bytes accessed | tf_op | source)
XLA Modules:
  0.0 250.6 jit_solution(14375220488236033558)
XLA Ops:
  0.6 0.0 copy-start
  0.6 0.0 copy-start.3
  0.7 0.0 copy-start.5
  0.7 0.0 copy-start.7
  0.7 0.0 copy-start.4
  0.7 1.1 copy.41
  1.8 0.3 eq.112
  2.1 0.5 fusion.36
  2.6 0.0 copy-done.3
  2.7 0.0 copy-done.5
  2.7 0.0 copy-done.7
  2.7 0.3 copy.39
  3.0 0.4 reshape.401
  3.4 0.0 copy-done.4
  3.4 0.2 copy.38
  3.6 0.3 reshape.400
  3.8 0.1 fusion.55
  3.9 0.1 copy.40
  4.0 0.1 broadcast_multiply_fusion
  4.1 0.9 fusion.39
  5.0 0.2 copy.42
  5.2 7.2 %push0.1 = s32[16,8,128]{2,1,0:T(8,128)S(1)} custom-call(s32[16,8,128]{2,1,0:T(8,128)S(1)} %get-tuple-element.25.refs_0_), custom_call_target="tpu_custom_call" | custom-call | tf_op jit(solution)/shard_map/push0/pallas_call | solution.py:80
  12.4 0.1 add_select_fusion
  12.5 2.9 %copy.37 = f32[8,512,128]{1,2,0:T(8,128)} copy(f32[8,512,128]{2,1,0:T(8,128)} %param.15) | data formatting | bytes 4194304 | tf_op args[5]
  15.3 8.7 %fusion.17 = bf16[8,2048,128]{2,1,0:T(8,128)(2,1)} fusion(s32[8,2048]{1,0:T(8,128)S(1)} %get-tuple-element.27, f32[8,512,128]{1,2,0:T(8,128)} %copy.37, pred[8,512]{1,0:T(8,128)(4,1)S(1)} %broadcast_compare_fusion), kind=kOutput, calls=%fused_computation.20 | convolution fusion | flops 2158493696 | bytes 6361088 | tf_op jit(solution)/shard_map/tbr,tre->tbe/dot_general | solution.py:279
  24.0 94.5 %push1.1 = bf16[8,16,128,128]{3,2,1,0:T(8,128)(2,1)S(1)} custom-call(bf16[8,16,128,128]{3,2,1,0:T(8,128)(2,1)} %bitcast.80), custom_call_target="tpu_custom_call" | custom-call | tf_op jit(solution)/shard_map/push1/pallas_call | solution.py:80
  118.6 0.0 copy-start.8
  118.6 2.1 fusion.33
  120.7 7.7 %all_gather.3 = bf16[128,2048]{0,1:T(8,128)(2,1)} all-gather(bf16[128,1024]{0,1:T(8,128)(2,1)S(1)} %bitcast.85), channel_id=1, replica_groups=mesh['dp'=16,'mp'=2] {'mp'}, dimensions={1}, use_global_device_ids=true | all-gather | bytes 786432 | tf_op jit(solution)/shard_map/all_gather | solution.py:291
  128.4 0.0 copy-start.9
  128.4 8.6 %all-to-all-start = ((bf16[16,128,128]{2,1,0:T(8,128)(2,1)}), bf16[16,128,128]{2,1,0:T(8,128)(2,1)}, u32[]{:S(2)}, u32[]{:S(2)}) async-start(bf16[16,128,128]{2,1,0:T(8,128)(2,1)} %bitcast.21), calls=%async_computation | async-start | bytes 1048576 | tf_op jit(solution)/shard_map/all_to_all | solution.py:307
  137.0 0.0 copy-done
  137.0 0.0 copy-done.8
  137.0 1.7 multiply_reduce_fusion.1
  138.7 4.4 %psum.7 = f32[128]{0:T(128)S(1)} all-reduce(f32[128]{0:T(128)S(1)} %get-tuple-element.34), channel_id=1, replica_groups=mesh['dp'=16,'mp'=2] {'mp'}, use_global_device_ids=true, to_apply=%region_3.4 | all-reduce | flops 128 | bytes 1024 | tf_op jit(solution)/shard_map/psum | solution.py:294
  143.1 0.0 copy-done.9
  143.1 0.0 copy-start.10
  143.1 0.1 multiply_convert_fusion.refs_0_
  143.2 0.8 convolution_convert_fusion
  144.0 0.3 copy.46
  144.3 0.0 copy-done.10
  144.3 0.2 copy.47
  144.5 6.8 %push2.1 = bf16[2,128,1024]{2,1,0:T(8,128)(2,1)S(1)} custom-call(bf16[2,128,1024]{2,1,0:T(8,128)(2,1)S(1)} %bitcast.79), custom_call_target="tpu_custom_call" | custom-call | tf_op jit(solution)/shard_map/push2/pallas_call | solution.py:80
  151.3 0.1 convert_reduce_fusion
  151.4 0.2 copy.48
  151.6 0.2 copy.49
  151.8 0.2 fusion.43.refs_1_
  152.0 48.6 %gather5.1 = (bf16[16,128,512]{2,1,0:T(8,128)(2,1)S(1)}, bf16[16,8,128,128]{3,2,1,0:T(8,128)(2,1)}) custom-call(bf16[128,512]{1,0:T(8,128)(2,1)S(1)} %multiply_convert_fusion.refs_0_, bf16[8,128,128]{2,1,0:T(8,128)(2,1)S(1)} %fusion.43.refs_1_), custom_call_target="tpu_custom_call" | custom-call | tf_op jit(solution)/shard_map/gather5/pallas_call | solution.py:203
  200.7 0.0 copy-start.1
  200.7 6.9 %fusion.18 = bf16[8,16,128,128]{3,2,1,0:T(8,128)(2,1)} fusion(bf16[16,8,128,128]{3,2,1,0:T(8,128)(2,1)} %get-tuple-element.6, s32[128]{0:T(128)S(1)} %iota_add_fusion, s32[8,16,128]{2,1,0:T(8,128)S(1)} %copy.43), kind=kOutput, calls=%fused_computation.21 | convolution fusion | flops 541065216 | bytes 8454656 | tf_op jit(solution)/shard_map/tgkn,gtne->tgke/dot_general | solution.py:310
  207.6 0.0 copy-done.1
  207.6 0.0 copy-start.6
  207.6 0.0 copy-start.2
  207.6 9.8 %multiply_reduce_fusion = (f32[8,512]{1,0:T(8,128)S(1)}, f32[8,512,128]{1,2,0:T(8,128)S(1)}) fusion(bf16[8,2048,128]{2,1,0:T(8,128)(2,1)} %bitcast.86, s32[8,2048]{1,0:T(8,128)S(1)} %get-tuple-element.27), kind=kOutput, calls=%fused_computation.24 | convolution fusion | flops 2156916736 | bytes 6373376 | tf_op jit(solution)/shard_map/trb,tbe->tre/dot_general | solution.py:317
  217.4 0.0 copy-done.6
  217.4 0.6 fusion.72
  218.0 0.0 copy-done.2
  218.0 1.9 divide_subtract_fusion
  219.9 2.9 %copy.52 = f32[8,512,128]{2,1,0:T(8,128)} copy(f32[8,512,128]{1,2,0:T(8,128)} %divide_subtract_fusion) | data formatting | bytes 4194304
  222.8 0.0 all-to-all-done
  222.8 2.2 fusion.40.refs_0_
  225.0 24.3 %gather4.1 = bf16[16,128,512]{2,1,0:T(8,128)(2,1)S(1)} custom-call(bf16[128,512]{1,0:T(8,128)(2,1)S(1)} %fusion.40.refs_0_), custom_call_target="tpu_custom_call" | custom-call | tf_op jit(solution)/shard_map/gather4/pallas_call | solution.py:203
  249.2 1.3 copy.61
  (11 shorter events, 0.1 us)
Async XLA Ops:
  0.6 136.4 %copy-start = (bf16[2048,512]{1,0:T(8,128)(2,1)S(1)}, bf16[2048,512]{1,0:T(8,128)(2,1)}, u32[]{:S(2)}) copy-start(bf16[2048,512]{1,0:T(8,128)(2,1)} %param.17) | copy-start | bytes 6291460
  0.6 2.0 copy-start.3
  0.7 2.0 copy-start.5
  0.7 2.0 copy-start.7
  0.7 2.7 %copy-start.4 = (s32[8,128,8]{1,2,0:T(8,128)S(1)}, s32[8,128,8]{1,2,0:T(8,128)}, u32[]{:S(2)}) copy-start(s32[8,128,8]{1,2,0:T(8,128)} %param.12) | copy-start | bytes 98308
  118.6 18.5 %copy-start.8 = (f32[512]{0:T(512)S(1)}, f32[512]{0:T(512)}, u32[]{:S(2)}) copy-start(f32[512]{0:T(512)} %param.18) | copy-start | bytes 6148
  128.4 14.7 %copy-start.9 = (s32[128]{0:T(128)S(1)}, s32[128]{0:T(128)}, u32[]{:S(2)}) copy-start(s32[128]{0:T(128)} %param.19) | copy-start | bytes 1540
  128.4 94.4 %all-to-all-start = ((bf16[16,128,128]{2,1,0:T(8,128)(2,1)}), bf16[16,128,128]{2,1,0:T(8,128)(2,1)}, u32[]{:S(2)}, u32[]{:S(2)}) async-start(bf16[16,128,128]{2,1,0:T(8,128)(2,1)} %bitcast.21), calls=%async_computation | async-start | bytes 1048576 | tf_op jit(solution)/shard_map/all_to_all | solution.py:307
  143.1 1.2 copy-start.10
  200.7 6.9 %copy-start.1 = (bf16[16,128,512]{2,1,0:T(8,128)(2,1)}, bf16[16,128,512]{2,1,0:T(8,128)(2,1)S(1)}, u32[]{:S(2)}) copy-start(bf16[16,128,512]{2,1,0:T(8,128)(2,1)S(1)} %get-tuple-element.7) | copy-start | bytes 6291460
  207.6 9.8 %copy-start.6 = (f32[8,512]{1,0:T(8,128)S(1)}, f32[8,512]{1,0:T(8,128)}, u32[]{:S(2)}) copy-start(f32[8,512]{1,0:T(8,128)} %param.16) | copy-start | bytes 49156
  207.6 10.4 %copy-start.2 = (f32[8,512,128]{1,2,0:T(8,128)S(1)}, f32[8,512,128]{1,2,0:T(8,128)}, u32[]{:S(2)}) copy-start(f32[8,512,128]{1,2,0:T(8,128)} %copy.37) | copy-start | bytes 6291460
